TPU v7x, 32 devices: a whole 2x2x4 slice. The times are simulated.
32 devices in a mesh: row: 8 (over z, x), col: 4 (over y, core).
Axes of the slice: x: 2, y: 2, z: 4, core: 2. Of those that a mesh axis runs over, the one named last changes fastest.
Arguments:
- homolog_stack: float32 [16, 64, 64], P(None, ('row', 'col')), may hold values from -6 to 6
- residue_grid: float32 [64, 64, 128], P('row', 'col'), may hold values from -6 to 27
- first_tensor_matrix: float32 [64, 32], replicated, may hold values from -0.75 to 0.75
- second_tensor_matrix: float32 [64, 32], replicated, may hold values from -0.75 to 0.75
- tensor_flatten_matrix: float32 [1024, 128], replicated, may hold values from -0.1875 to 0.1875
- tensor_offset_vector: float32 [128], replicated, may hold values from -3 to 3
- feedforward_switch_matrix: float32 [128, 512], replicated, may hold values from -0.5 to 0.5
- expand_matrix: float32 [128, 512], replicated, may hold values from -0.5 to 0.5
- shrink_matrix: float32 [512, 128], replicated, may hold values from -0.25 to 0.25
- grid_score_matrix: float32 [128, 8], replicated, may hold values from -48 to 48
- homolog_content_matrix: float32 [64, 256], replicated, may hold values from -0.75 to 0.75
- homolog_sigmoid_matrix: float32 [64, 256], replicated, may hold values from -0.75 to 0.75
- mixing_result_matrix: float32 [256, 64], replicated, may hold values from -0.375 to 0.375
Outputs:
- pair_output: float32 [64, 64, 128], P('row', 'col')
- homolog_refreshed: float32 [16, 64, 64], P(None, ('row', 'col'))
All inputs are finite; a program needn't handle non-finite values.
Results may differ from a plain program's by a relative error of at most 0.00029.
Values sent between devices are 32-bit elements; how exact they have to be, the bound alone decides.
A program may use at most 64 MiB of HBM per device.

v0:
```python
import functools

import jax
import jax.numpy as jnp
from jax import lax
from jax.experimental import pallas as pl
from jax.experimental.pallas import tpu as pltpu
from jax.sharding import PartitionSpec as P

epsilon = 1e-05
MESH = pl.DeviceIdType.MESH
f32 = jnp.float32
bf16 = jnp.bfloat16


def split(x):
    hi = x.astype(bf16)
    return hi, (x - hi.astype(f32)).astype(bf16)


def mm(a, b):
    return jnp.dot(a, b, preferred_element_type=f32)


def standardize(x):
    centered = x - jnp.mean(x, axis=-1, keepdims=True)
    return centered * lax.rsqrt(jnp.mean(centered * centered, axis=-1, keepdims=True) + epsilon)


def stacked(x):
    hi, lo = split(x)
    return jnp.concatenate([hi, lo, hi], axis=1)


def stacked_rows(w):
    hi, lo = split(w)
    return jnp.concatenate([hi, hi, lo], axis=0)


def kernel(dims, *refs):
    (R, C, S, TP, I, J, IB) = dims
    (x_h, res_h, fst_h, snd_h, flat_h, off_h, sw_h, ex_h, sh_h, gs_h, ct_h, sg_h, mx_h) = refs[:13]
    (pair, mixed_o, mstk, x_o) = refs[13:17]
    (x, res, fst, snd, flat, off, sw, ex, sh, gs, ct, sg, mx) = refs[17:30]
    (rowbuf, colbuf, frep, srep, cstk, wf, wg_hh, wg_l, wsh, grep, l2, r2, vals, ohl, w2,
     part, got, wide, mixbuf, in_sem, send_sem, row_sem, col_sem, psend, precv) = refs[30:]
    r, c = lax.axis_index("row"), lax.axis_index("col")
    lin = r * C + c
    B = S * TP
    CD = flat.shape[0]
    D = fst.shape[0]
    HC = ct.shape[1]
    H = gs.shape[0]
    Z = flat.shape[1]
    FF = sw.shape[1]
    F = fst.shape[1]

    barrier = pltpu.get_barrier_semaphore()
    c_dst = lin // R
    slot = lax.rem(lin, R)
    own = c_dst == c

    def greet(a, b):
        pl.semaphore_signal(barrier, inc=1, device_id=(a, b), device_id_type=MESH)

    copies = []
    for n, (src, dst) in enumerate(zip(
        (x_h, fst_h, snd_h, ct_h, sg_h, gs_h, flat_h, off_h, res_h, sw_h, ex_h, sh_h, mx_h),
        (x, fst, snd, ct, sg, gs, flat, off, res, sw, ex, sh, mx))):
        cp = pltpu.make_async_copy(src, dst, in_sem.at[n])
        cp.start()
        copies.append(cp)
    (cx, cfst, csnd, cct, csg, cgs, cflat, coff, cres, csw, cex, csh, cmx) = copies

    for k in range(1, C):
        greet(r, lax.rem(c + k, C))
    for k in range(1, R):
        greet(lax.rem(r + k, R), c_dst)

    @pl.when(jnp.logical_not(own))
    def _():
        greet(r, c_dst)

    for k in range(R):
        src = c * R + k

        @pl.when(src != lin)
        def _():
            greet(src // C, lax.rem(src, C))

    self_in = jnp.where(own, 1, 0)
    cx.wait()
    pl.semaphore_wait(barrier, (C - 1) + 2 * (R - self_in))

    def row_copy(to, at, n):
        return pltpu.make_async_remote_copy(
            src_ref=x, dst_ref=rowbuf.at[pl.ds(pl.multiple_of(at * B, B), B)],
            send_sem=send_sem.at[n], recv_sem=row_sem.at[at],
            device_id=(r, to), device_id_type=MESH)

    def col_copy(to, at, n):
        return pltpu.make_async_remote_copy(
            src_ref=x, dst_ref=colbuf.at[pl.ds(pl.multiple_of(at * B, B), B)],
            send_sem=send_sem.at[n], recv_sem=col_sem.at[at],
            device_id=(to, c_dst), device_id_type=MESH)

    for k in range(1, R):
        col_copy(lax.rem(r + k, R), slot, C + k).start()

    @pl.when(jnp.logical_not(own))
    def _():
        col_copy(r, slot, C).start()

    for k in range(1, C):
        row_copy(lax.rem(c + k, C), c, k).start()

    mine = x[...]
    x_o[...] = mine
    rowbuf[pl.ds(pl.multiple_of(c * B, B), B), :] = mine

    @pl.when(own)
    def _():
        colbuf[pl.ds(pl.multiple_of(slot * B, B), B), :] = mine

    lane = lax.broadcasted_iota(jnp.int32, (D, CD), 1)
    sub = lax.broadcasted_iota(jnp.int32, (D, CD), 0)
    rep_of = jnp.where(lane // D == sub, 1.0, 0.0).astype(bf16)
    tile_of = jnp.where(lax.rem(lane, D) == sub, 1.0, 0.0).astype(bf16)
    for cp, w, e, out in ((cfst, fst, rep_of, frep), (csnd, snd, tile_of, srep)):
        cp.wait()
        hi, lo = split(w[...].T)
        hi = mm(hi, e).astype(bf16)
        out[0:F, :] = hi
        out[F:2 * F, :] = hi
        out[2 * F:3 * F, :] = mm(lo, e).astype(bf16)
    cct.wait()
    cstk[...] = stacked_rows(ct[...])
    cgs.wait()
    head = lax.broadcasted_iota(jnp.int32, (H, HC), 1) // (HC // H)
    spread = jnp.where(head == lax.broadcasted_iota(jnp.int32, (H, HC), 0), 1.0, 0.0).astype(f32)
    grep[...] = jnp.dot(gs[...].T, spread, precision=lax.Precision.HIGHEST, preferred_element_type=f32)
    cflat.wait()
    hi, lo = split(flat[...])
    wf[:, 0:Z] = hi
    wf[:, Z:2 * Z] = lo
    for cp, w, at in ((csw, sw, 0), (cex, ex, FF)):
        cp.wait()
        hi, lo = split(w[...])
        wg_hh[0:Z, at:at + FF] = hi
        wg_hh[Z:2 * Z, at:at + FF] = hi
        wg_l[:, at:at + FF] = lo
    csh.wait()
    hi, lo = split(sh[...])
    wsh[:, 0:Z] = hi
    wsh[:, Z:2 * Z] = lo
    cmx.wait()
    mstk[...] = stacked_rows(mx[...].T)
    csg.wait()
    gate = jax.nn.sigmoid(mm(stacked(standardize(mine)), stacked_rows(sg[...])))

    for k in range(C):
        @pl.when(k != c)
        def _():
            row_copy(c, k, 0).wait_recv()
    l2[...] = mm(stacked(standardize(rowbuf[...])), frep[...]) * (1.0 / S)
    for k in range(R):
        @pl.when(c * R + k != lin)
        def _():
            col_copy(r, k, 0).wait_recv()
    cols = standardize(colbuf[...])
    wide[...] = jnp.concatenate([cols, jnp.zeros((R * B, wide.shape[1] - F), f32)], axis=1)
    cols = jnp.concatenate(
        [wide[pl.ds(s * TP + t, R, stride=B), :] for s in range(S) for t in range(TP)], axis=0)
    cols = stacked(cols[:, 0:F])
    r2[...] = mm(cols, srep[...])
    values = mm(cols, cstk[...])
    for h in range(HC // 128):
        vals[h] = values[:, h * 128:(h + 1) * 128]
    coff.wait()
    cres.wait()

    NP = IB * J

    def chunk(i0):
        if I == IB:
            l2c, resc, pairc = l2, res, pair
        else:
            l2c = l2.at[pl.ds(pl.multiple_of((i0 // TP) * B, B), (IB // TP) * B)]
            rows = pl.ds(pl.multiple_of(i0 * J, IB * J), IB * J)
            resc, pairc = res.at[rows], pair.at[rows]

        def lanes_step(lt, carry):
            at = pl.ds(pl.multiple_of(lt * 128, 128), 128)
            acc = [None] * IB
            for s in range(S):
                right = r2[s * J:(s + 1) * J, at]
                for ii in range(IB):
                    left = l2c[pl.ds((ii // TP) * B + s * TP + ii % TP, 1), at]
                    term = left * right
                    acc[ii] = term if s == 0 else acc[ii] + term
            for ii in range(IB):
                hi, lo = split(acc[ii])
                ohl[ii * J:(ii + 1) * J, at] = hi
                ohl[NP + ii * J:NP + (ii + 1) * J, at] = lo
            return carry

        lax.fori_loop(0, CD // 128, lanes_step, 0)
        up = mm(ohl[...], wf[...])
        update = up[0:NP, 0:Z] + (up[NP:, 0:Z] + up[0:NP, Z:])
        base = jnp.concatenate(
            [resc[pl.ds(ii * J + t, R, stride=TP), :] for ii in range(IB) for t in range(TP)], axis=0)
        mid = base + (update + off[...])
        hi, lo = split(standardize(mid))
        hid = mm(jnp.concatenate([hi, lo], axis=1), wg_hh[...]) + mm(hi, wg_l[...])
        g = hid[:, 0:FF]
        hidden = g / (1.0 + jnp.exp(-g)) * hid[:, FF:]
        hi, lo = split(hidden)
        down = mm(jnp.concatenate([hi, lo], axis=0), wsh[...])
        new = mid + (down[0:NP, 0:Z] + (down[NP:, 0:Z] + down[0:NP, Z:]))
        for ii in range(IB):
            for t in range(TP):
                a = (ii * TP + t) * R
                pairc[pl.ds(ii * J + t, R, stride=TP), :] = new[a:a + R, :]
        logits = jnp.dot(standardize(new), grep[...], precision=lax.Precision.HIGHEST,
                         preferred_element_type=f32)
        for ii in range(IB):
            i = i0 + ii
            row = logits[ii * J:(ii + 1) * J, :]
            peak = jnp.max(row, axis=0, keepdims=True)
            e = jnp.exp(row - peak)
            w2[ii * J:(ii + 1) * J, :] = e
            total = jnp.sum(e, axis=0, keepdims=True)
            which = lax.broadcasted_iota(jnp.int32, (8, HC), 0)
            part[i, S:S + 8, :] = jnp.where(which == 0, total, peak)
        for ii in range(IB):
            for h in range(HC // 128):
                at = slice(h * 128, (h + 1) * 128)
                acc = None
                for j in range(J):
                    term = w2[pl.ds(ii * J + j, 1), at] * vals[h, pl.ds(j, S, stride=J), :]
                    acc = term if acc is None else acc + term
                part[i0 + ii, 0:S, at] = acc

    if I == IB:
        chunk(0)
    else:
        def step(n, carry):
            chunk(n * IB)
            return carry
        lax.fori_loop(0, I // IB, step, 0)

    def part_copy(to, at, n):
        return pltpu.make_async_remote_copy(
            src_ref=part.at[pl.ds(to * TP, TP)], dst_ref=got.at[pl.ds(at * TP, TP)],
            send_sem=psend.at[n], recv_sem=precv.at[at],
            device_id=(r, to), device_id_type=MESH)

    for k in range(1, C):
        part_copy(lax.rem(c + k, C), c, k).start()
    got[pl.ds(c * TP, TP)] = part[pl.ds(c * TP, TP)]

    for k in range(1, R):
        col_copy(lax.rem(r + k, R), slot, C + k).wait_send()

    @pl.when(jnp.logical_not(own))
    def _():
        col_copy(r, slot, C).wait_send()

    for k in range(1, C):
        row_copy(lax.rem(c + k, C), c, k).wait_send()

    for k in range(C):
        @pl.when(k != c)
        def _():
            part_copy(c, k, 0).wait_recv()

    for t in range(TP):
        peaks = [got[k * TP + t, S + 1:S + 2, :] for k in range(C)]
        top = functools.reduce(jnp.maximum, peaks)
        scale = [jnp.exp(p - top) for p in peaks]
        total = sum(got[k * TP + t, S:S + 1, :] * scale[k] for k in range(C))
        summed = sum(got[k * TP + t, 0:S, :] * scale[k] for k in range(C))
        summed = summed / total
        for h in range(HC // 128):
            mixbuf[h, pl.ds(t, S, stride=TP), :] = summed[:, h * 128:(h + 1) * 128]
    mixed_o[...] = gate * jnp.concatenate([mixbuf[h] for h in range(HC // 128)], axis=1)
    for k in range(1, C):
        part_copy(lax.rem(c + k, C), c, k).wait_send()


def finish(pair, mixed, mstk, x, pair_h, hom_o, sem):
    out = pltpu.make_async_copy(pair, pair_h, sem)
    out.start()
    hom_o[...] = x[...] + mm(stacked(mixed[...]), mstk[...])
    out.wait()


def on_device(R, C, homolog_stack, residue_grid, first, second, flatten, offset, switch, expand,
              shrink, score, content, sig, mixing):
    S, TP, F = homolog_stack.shape
    I, J, Z = residue_grid.shape
    IB = max(TP, min(I, 128 // J))
    NP = IB * J
    CD = flatten.shape[0]
    FF = switch.shape[1]
    HC = content.shape[1]
    B = S * TP
    args = (homolog_stack.reshape(B, F), residue_grid.reshape(I * J, Z), first.T, second.T, flatten,
            offset.reshape(1, Z), switch, expand, shrink, score.T, content, sig, mixing.T)
    args = tuple(pltpu.with_memory_space_constraint(a, pltpu.HBM) for a in args)
    dma = pltpu.SemaphoreType.DMA
    pair, mixed, mstk, kept = pl.pallas_call(
        functools.partial(kernel, (R, C, S, TP, I, J, IB)),
        out_shape=(jax.ShapeDtypeStruct((I * J, Z), f32), jax.ShapeDtypeStruct((B, HC), f32),
                   jax.ShapeDtypeStruct((3 * HC, F), bf16), jax.ShapeDtypeStruct((B, F), f32)),
        in_specs=[pl.BlockSpec(memory_space=pltpu.HBM)] * 13,
        out_specs=[pl.BlockSpec(memory_space=pltpu.VMEM)] * 4,
        scratch_shapes=[pltpu.VMEM(a.shape, f32) for a in args] + [
            pltpu.VMEM((C * B, F), f32),
            pltpu.VMEM((R * B, F), f32),
            pltpu.VMEM((3 * F, CD), bf16),
            pltpu.VMEM((3 * F, CD), bf16),
            pltpu.VMEM((3 * F, HC), bf16),
            pltpu.VMEM((CD, 2 * Z), bf16),
            pltpu.VMEM((2 * Z, 2 * FF), bf16),
            pltpu.VMEM((Z, 2 * FF), bf16),
            pltpu.VMEM((FF, 2 * Z), bf16),
            pltpu.VMEM((Z, HC), f32),
            pltpu.VMEM((C * B, CD), f32),
            pltpu.VMEM((S * J, CD), f32),
            pltpu.VMEM((HC // 128, S * J, 128), f32),
            pltpu.VMEM((2 * NP, CD), bf16),
            pltpu.VMEM((NP, HC), f32),
            pltpu.VMEM((I, S + 8, HC), f32),
            pltpu.VMEM((I, S + 8, HC), f32),
            pltpu.VMEM((R * B, 128), f32),
            pltpu.VMEM((HC // 128, B, 128), f32),
            dma((13,)), dma((C + R,)), dma((C,)), dma((R,)), dma((C,)), dma((C,)),
        ],
        compiler_params=pltpu.CompilerParams(
            collective_id=0, has_side_effects=True, vmem_limit_bytes=32 * 1024 * 1024),
        name="msa_block",
    )(*args)
    pair, hom = pl.pallas_call(
        finish,
        out_shape=(jax.ShapeDtypeStruct((I * J, Z), f32), jax.ShapeDtypeStruct((B, F), f32)),
        in_specs=[pl.BlockSpec(memory_space=pltpu.VMEM)] * 4,
        out_specs=(pl.BlockSpec(memory_space=pltpu.HBM), pl.BlockSpec(memory_space=pltpu.VMEM)),
        scratch_shapes=[dma(())],
        compiler_params=pltpu.CompilerParams(vmem_limit_bytes=16 * 1024 * 1024),
        name="msa_finish",
    )(pair, mixed, mstk, kept)
    return pair.reshape(I, J, Z), hom.reshape(S, TP, F)


def solution(mesh):
    R, C = mesh.shape["row"], mesh.shape["col"]
    return jax.shard_map(
        functools.partial(on_device, R, C),
        mesh=mesh,
        in_specs=(P(None, ("row", "col"), None), P("row", "col", None)) + (P(),) * 11,
        out_specs=(P("row", "col", None), P(None, ("row", "col"), None)),
        check_vma=False,
    )
```

profile of v0, /device:TPU:0, one launch (start us, length us, event | category | flops | bytes accessed | tf_op | source)
XLA Modules:
  0.0 19.9 jit_solution(12720595372699187361)
XLA Ops:
  0.6 18.0 %msa_block.1 = (f32[128,128]{1,0:T(8,128)S(1)}, f32[32,256]{1,0:T(8,128)S(1)}, bf16[768,64]{1,0:T(8,128)(2,1)S(1)}, f32[32,64]{1,0:T(8,128)S(1)}) custom-call(f32[32,64]{1,0:T(8,128)} %bitcast.11, f32[128,128]{1,0:T(8,128)} %bitcast.9, f32[32,64]{1,0:T(8,128)} %bitcast.12, f32[32,64]{1,0:T(8,128)} %bitcast.13, f32[1024,128]{1,0:T(8,128)} %refs_4_.1, ...), custom_call_target="tpu_custom_call" | custom-call | tf_op jit(solution)/shard_map/msa_block/pallas_call | solution.py:312
  18.6 1.3 %msa_finish.1 = (f32[128,128]{1,0:T(8,128)}, f32[32,64]{1,0:T(8,128)}) custom-call(f32[128,128]{1,0:T(8,128)S(1)} %get-tuple-element.8.pair, f32[32,256]{1,0:T(8,128)S(1)} %get-tuple-element.9.mixed, bf16[768,64]{1,0:T(8,128)(2,1)S(1)} %get-tuple-element.10.mstk, f32[32,64]{1,0:T(8,128)S(1)} %get-tuple-element.11.x), custom_call_target="tpu_custom_call" | custom-call | tf_op jit(solution)/shard_map/msa_finish/pallas_call | solution.py:344
where the time goes:
time: 20.1 us; the launch traced here: 19.9 us
  Pallas kernels  19.2 us (96%)
  between operations  0.64 us (3%)
    pallas_call x1, Pallas kernels, on_device(): pl.pallas_call(functools.partial(kernel, (R, C, S, TP, I, J, IB)), out_sh...  18 us
    pallas_call x1, Pallas kernels, on_device(): pl.pallas_call(finish, out_shape=(jax.ShapeDtypeStruct((I * J, Z), f32),...  1.27 us

commit v1 on v0

--- a/solution.py
+++ b/solution.py
@@ -43,7 +43,7 @@
     (pair, mixed_o, mstk, x_o) = refs[13:17]
     (x, res, fst, snd, flat, off, sw, ex, sh, gs, ct, sg, mx) = refs[17:30]
     (rowbuf, colbuf, frep, srep, cstk, wf, wg_hh, wg_l, wsh, grep, l2, r2, vals, ohl, w2,
-     part, got, wide, mixbuf, in_sem, send_sem, row_sem, col_sem, psend, precv) = refs[30:]
+     part, stat, got, got_stat, wide, packed, mixbuf, in_sem, send_sem, row_sem, col_sem, psend, precv, ssend, srecv) = refs[30:]
     r, c = lax.axis_index("row"), lax.axis_index("col")
     lin = r * C + c
     B = S * TP
@@ -90,17 +90,19 @@
 
     self_in = jnp.where(own, 1, 0)
     cx.wait()
+    wide[...] = jnp.concatenate([x[...], jnp.zeros((B, 128 - F), f32)], axis=1)
+    packed[...] = jnp.concatenate([wide[pl.ds(t, S, stride=TP), :][:, 0:F] for t in range(TP)], axis=1)
     pl.semaphore_wait(barrier, (C - 1) + 2 * (R - self_in))
 
     def row_copy(to, at, n):
         return pltpu.make_async_remote_copy(
-            src_ref=x, dst_ref=rowbuf.at[pl.ds(pl.multiple_of(at * B, B), B)],
+            src_ref=packed, dst_ref=rowbuf.at[pl.ds(pl.multiple_of(at * S, S), S)],
             send_sem=send_sem.at[n], recv_sem=row_sem.at[at],
             device_id=(r, to), device_id_type=MESH)
 
     def col_copy(to, at, n):
         return pltpu.make_async_remote_copy(
-            src_ref=x, dst_ref=colbuf.at[pl.ds(pl.multiple_of(at * B, B), B)],
+            src_ref=packed, dst_ref=colbuf.at[pl.ds(pl.multiple_of(at * S, S), S)],
             send_sem=send_sem.at[n], recv_sem=col_sem.at[at],
             device_id=(to, c_dst), device_id_type=MESH)
 
@@ -116,11 +118,11 @@
 
     mine = x[...]
     x_o[...] = mine
-    rowbuf[pl.ds(pl.multiple_of(c * B, B), B), :] = mine
+    rowbuf[pl.ds(pl.multiple_of(c * S, S), S), :] = packed[...]
 
     @pl.when(own)
     def _():
-        colbuf[pl.ds(pl.multiple_of(slot * B, B), B), :] = mine
+        colbuf[pl.ds(pl.multiple_of(slot * S, S), S), :] = packed[...]
 
     lane = lax.broadcasted_iota(jnp.int32, (D, CD), 1)
     sub = lax.broadcasted_iota(jnp.int32, (D, CD), 0)
@@ -162,16 +164,17 @@
         @pl.when(k != c)
         def _():
             row_copy(c, k, 0).wait_recv()
-    l2[...] = mm(stacked(standardize(rowbuf[...])), frep[...]) * (1.0 / S)
+
+    def tokens(block):
+        return jnp.concatenate([standardize(block[:, t * F:(t + 1) * F]) for t in range(TP)], axis=0)
+
+    l2[...] = mm(stacked(tokens(rowbuf[...])), frep[...]) * (1.0 / S)
     for k in range(R):
         @pl.when(c * R + k != lin)
         def _():
             col_copy(r, k, 0).wait_recv()
-    cols = standardize(colbuf[...])
-    wide[...] = jnp.concatenate([cols, jnp.zeros((R * B, wide.shape[1] - F), f32)], axis=1)
-    cols = jnp.concatenate(
-        [wide[pl.ds(s * TP + t, R, stride=B), :] for s in range(S) for t in range(TP)], axis=0)
-    cols = stacked(cols[:, 0:F])
+    cols = stacked(tokens(jnp.concatenate(
+        [colbuf[pl.ds(s, R, stride=S), :] for s in range(S)], axis=0)))
     r2[...] = mm(cols, srep[...])
     values = mm(cols, cstk[...])
     for h in range(HC // 128):
@@ -181,21 +184,32 @@
 
     NP = IB * J
 
+    def part_copy(to, at):
+        return pltpu.make_async_remote_copy(
+            src_ref=part.at[pl.ds(to * TP, TP)], dst_ref=got.at[pl.ds(at * TP, TP)],
+            send_sem=psend.at[to], recv_sem=precv.at[at],
+            device_id=(r, to), device_id_type=MESH)
+
+    def stat_copy(to, at):
+        return pltpu.make_async_remote_copy(
+            src_ref=stat.at[to], dst_ref=got_stat.at[at],
+            send_sem=ssend.at[to], recv_sem=srecv.at[at],
+            device_id=(r, to), device_id_type=MESH)
+
     def chunk(i0):
-        if I == IB:
-            l2c, resc, pairc = l2, res, pair
-        else:
-            l2c = l2.at[pl.ds(pl.multiple_of((i0 // TP) * B, B), (IB // TP) * B)]
-            rows = pl.ds(pl.multiple_of(i0 * J, IB * J), IB * J)
-            resc, pairc = res.at[rows], pair.at[rows]
+        d0 = i0 // TP
+        l2c = [l2.at[pl.ds(pl.multiple_of((t * C + d0) * S, S), (IB // TP) * S)] for t in range(TP)]
+        rows = pl.ds(pl.multiple_of(i0 * J, IB * J), IB * J)
+        resc, pairc = res.at[rows], pair.at[rows]
 
         def lanes_step(lt, carry):
             at = pl.ds(pl.multiple_of(lt * 128, 128), 128)
             acc = [None] * IB
             for s in range(S):
-                right = r2[s * J:(s + 1) * J, at]
+                right = jnp.concatenate(
+                    [r2[(t * S + s) * R:(t * S + s + 1) * R, at] for t in range(TP)], axis=0)
                 for ii in range(IB):
-                    left = l2c[pl.ds((ii // TP) * B + s * TP + ii % TP, 1), at]
+                    left = l2c[ii % TP][pl.ds((ii // TP) * S + s, 1), at]
                     term = left * right
                     acc[ii] = term if s == 0 else acc[ii] + term
             for ii in range(IB):
@@ -223,41 +237,44 @@
                 pairc[pl.ds(ii * J + t, R, stride=TP), :] = new[a:a + R, :]
         logits = jnp.dot(standardize(new), grep[...], precision=lax.Precision.HIGHEST,
                          preferred_element_type=f32)
-        for ii in range(IB):
-            i = i0 + ii
-            row = logits[ii * J:(ii + 1) * J, :]
-            peak = jnp.max(row, axis=0, keepdims=True)
-            e = jnp.exp(row - peak)
-            w2[ii * J:(ii + 1) * J, :] = e
-            total = jnp.sum(e, axis=0, keepdims=True)
-            which = lax.broadcasted_iota(jnp.int32, (8, HC), 0)
-            part[i, S:S + 8, :] = jnp.where(which == 0, total, peak)
+        for d in range(IB // TP):
+            notes = []
+            for t in range(TP):
+                ii = d * TP + t
+                row = logits[ii * J:(ii + 1) * J, :]
+                peak = jnp.max(row, axis=0, keepdims=True)
+                e = jnp.exp(row - peak)
+                w2[ii * J:(ii + 1) * J, :] = e
+                notes += [jnp.sum(e, axis=0, keepdims=True), peak]
+            notes.append(jnp.zeros((8 - 2 * TP, HC), f32))
+            stat[d0 + d] = jnp.concatenate(notes, axis=0)
         for ii in range(IB):
             for h in range(HC // 128):
                 at = slice(h * 128, (h + 1) * 128)
                 acc = None
                 for j in range(J):
-                    term = w2[pl.ds(ii * J + j, 1), at] * vals[h, pl.ds(j, S, stride=J), :]
+                    term = w2[pl.ds(ii * J + j, 1), at] * vals[h, pl.ds((j // R) * S * R + j % R, S, stride=R), :]
                     acc = term if acc is None else acc + term
-                part[i0 + ii, 0:S, at] = acc
-
-    if I == IB:
-        chunk(0)
+                part[i0 + ii, :, at] = acc
+        for d in range(IB // TP):
+            @pl.when(d0 + d != c)
+            def _():
+                part_copy(d0 + d, c).start()
+                stat_copy(d0 + d, c).start()
+
+    count = I // IB
+    last = (c * TP) // IB
+    if count <= 2:
+        for n in range(count):
+            chunk(lax.rem(last + 1 + n, count) * IB)
     else:
         def step(n, carry):
-            chunk(n * IB)
+            chunk(lax.rem(last + 1 + n, count) * IB)
             return carry
-        lax.fori_loop(0, I // IB, step, 0)
-
-    def part_copy(to, at, n):
-        return pltpu.make_async_remote_copy(
-            src_ref=part.at[pl.ds(to * TP, TP)], dst_ref=got.at[pl.ds(at * TP, TP)],
-            send_sem=psend.at[n], recv_sem=precv.at[at],
-            device_id=(r, to), device_id_type=MESH)
-
-    for k in range(1, C):
-        part_copy(lax.rem(c + k, C), c, k).start()
+        lax.fori_loop(0, count, step, 0)
+
     got[pl.ds(c * TP, TP)] = part[pl.ds(c * TP, TP)]
+    got_stat[c] = stat[c]
 
     for k in range(1, R):
         col_copy(lax.rem(r + k, R), slot, C + k).wait_send()
@@ -272,20 +289,22 @@
     for k in range(C):
         @pl.when(k != c)
         def _():
-            part_copy(c, k, 0).wait_recv()
+            part_copy(c, k).wait_recv()
+            stat_copy(c, k).wait_recv()
 
     for t in range(TP):
-        peaks = [got[k * TP + t, S + 1:S + 2, :] for k in range(C)]
+        peaks = [got_stat[k, 2 * t + 1:2 * t + 2, :] for k in range(C)]
         top = functools.reduce(jnp.maximum, peaks)
         scale = [jnp.exp(p - top) for p in peaks]
-        total = sum(got[k * TP + t, S:S + 1, :] * scale[k] for k in range(C))
-        summed = sum(got[k * TP + t, 0:S, :] * scale[k] for k in range(C))
+        total = sum(got_stat[k, 2 * t:2 * t + 1, :] * scale[k] for k in range(C))
+        summed = sum(got[k * TP + t] * scale[k] for k in range(C))
         summed = summed / total
         for h in range(HC // 128):
             mixbuf[h, pl.ds(t, S, stride=TP), :] = summed[:, h * 128:(h + 1) * 128]
     mixed_o[...] = gate * jnp.concatenate([mixbuf[h] for h in range(HC // 128)], axis=1)
     for k in range(1, C):
-        part_copy(lax.rem(c + k, C), c, k).wait_send()
+        part_copy(lax.rem(c + k, C), c).wait_send()
+        stat_copy(lax.rem(c + k, C), c).wait_send()
 
 
 def finish(pair, mixed, mstk, x, pair_h, hom_o, sem):
@@ -299,7 +318,7 @@
               shrink, score, content, sig, mixing):
     S, TP, F = homolog_stack.shape
     I, J, Z = residue_grid.shape
-    IB = max(TP, min(I, 128 // J))
+    IB = max(TP, min(I // 2, 64 // J))
     NP = IB * J
     CD = flatten.shape[0]
     FF = switch.shape[1]
@@ -316,8 +335,8 @@
         in_specs=[pl.BlockSpec(memory_space=pltpu.HBM)] * 13,
         out_specs=[pl.BlockSpec(memory_space=pltpu.VMEM)] * 4,
         scratch_shapes=[pltpu.VMEM(a.shape, f32) for a in args] + [
-            pltpu.VMEM((C * B, F), f32),
-            pltpu.VMEM((R * B, F), f32),
+            pltpu.VMEM((C * S, TP * F), f32),
+            pltpu.VMEM((R * S, TP * F), f32),
             pltpu.VMEM((3 * F, CD), bf16),
             pltpu.VMEM((3 * F, CD), bf16),
             pltpu.VMEM((3 * F, HC), bf16),
@@ -331,11 +350,14 @@
             pltpu.VMEM((HC // 128, S * J, 128), f32),
             pltpu.VMEM((2 * NP, CD), bf16),
             pltpu.VMEM((NP, HC), f32),
-            pltpu.VMEM((I, S + 8, HC), f32),
-            pltpu.VMEM((I, S + 8, HC), f32),
-            pltpu.VMEM((R * B, 128), f32),
+            pltpu.VMEM((I, S, HC), f32),
+            pltpu.VMEM((C, 8, HC), f32),
+            pltpu.VMEM((I, S, HC), f32),
+            pltpu.VMEM((C, 8, HC), f32),
+            pltpu.VMEM((B, 128), f32),
+            pltpu.VMEM((S, TP * F), f32),
             pltpu.VMEM((HC // 128, B, 128), f32),
-            dma((13,)), dma((C + R,)), dma((C,)), dma((R,)), dma((C,)), dma((C,)),
+            dma((13,)), dma((C + R,)), dma((C,)), dma((R,)), dma((C,)), dma((C,)), dma((C,)), dma((C,)),
         ],
         compiler_params=pltpu.CompilerParams(
             collective_id=0, has_side_effects=True, vmem_limit_bytes=32 * 1024 * 1024),

time: 20.1 us -> 18.5 us (0.920)
  Pallas kernels: 19.2 us -> 17.6 us
    pallas_call x1, Pallas kernels: 18 us -> 16.3 us  [on_device(): pl.pallas_call(functools.partial(kernel, (R, C, S, TP, I, J, IB)), out_sh...]
where the time goes in v1:
time: 18.5 us; the launch traced here: 18.3 us
  Pallas kernels  17.6 us (95%)
  between operations  0.64 us (3%)
    pallas_call x1, Pallas kernels, on_device(): pl.pallas_call(functools.partial(kernel, (R, C, S, TP, I, J, IB)), out_sh...  16.3 us
    pallas_call x1, Pallas kernels, on_device(): pl.pallas_call(finish, out_shape=(jax.ShapeDtypeStruct((I * J, Z), f32),...  1.27 us

profile of v1, /device:TPU:0, one launch (start us, length us, event | category | flops | bytes accessed | tf_op | source)
XLA Modules:
  0.0 18.3 jit_solution(4090767156861348566)
XLA Ops:
  0.6 16.3 %msa_block.1 = (f32[128,128]{1,0:T(8,128)S(1)}, f32[32,256]{1,0:T(8,128)S(1)}, bf16[768,64]{1,0:T(8,128)(2,1)S(1)}, f32[32,64]{1,0:T(8,128)S(1)}) custom-call(f32[32,64]{1,0:T(8,128)} %bitcast.11, f32[128,128]{1,0:T(8,128)} %bitcast.9, f32[32,64]{1,0:T(8,128)} %bitcast.12, f32[32,64]{1,0:T(8,128)} %bitcast.13, f32[1024,128]{1,0:T(8,128)} %refs_4_.1, ...), custom_call_target="tpu_custom_call" | custom-call | tf_op jit(solution)/shard_map/msa_block/pallas_call | solution.py:331
  17.0 1.3 %msa_finish.1 = (f32[128,128]{1,0:T(8,128)}, f32[32,64]{1,0:T(8,128)}) custom-call(f32[128,128]{1,0:T(8,128)S(1)} %get-tuple-element.8.pair, f32[32,256]{1,0:T(8,128)S(1)} %get-tuple-element.9.mixed, bf16[768,64]{1,0:T(8,128)(2,1)S(1)} %get-tuple-element.10.mstk, f32[32,64]{1,0:T(8,128)S(1)} %get-tuple-element.11.x), custom_call_target="tpu_custom_call" | custom-call | tf_op jit(solution)/shard_map/msa_finish/pallas_call | solution.py:366

commit v2 on v1

--- a/solution.py
+++ b/solution.py
@@ -218,7 +218,7 @@
                 ohl[NP + ii * J:NP + (ii + 1) * J, at] = lo
             return carry
 
-        lax.fori_loop(0, CD // 128, lanes_step, 0)
+        lax.fori_loop(0, CD // 128, lanes_step, 0, unroll=4)
         up = mm(ohl[...], wf[...])
         update = up[0:NP, 0:Z] + (up[NP:, 0:Z] + up[0:NP, Z:])
         base = jnp.concatenate(
@@ -248,15 +248,16 @@
                 notes += [jnp.sum(e, axis=0, keepdims=True), peak]
             notes.append(jnp.zeros((8 - 2 * TP, HC), f32))
             stat[d0 + d] = jnp.concatenate(notes, axis=0)
-        for ii in range(IB):
-            for h in range(HC // 128):
-                at = slice(h * 128, (h + 1) * 128)
-                acc = None
-                for j in range(J):
-                    term = w2[pl.ds(ii * J + j, 1), at] * vals[h, pl.ds((j // R) * S * R + j % R, S, stride=R), :]
-                    acc = term if acc is None else acc + term
-                part[i0 + ii, :, at] = acc
         for d in range(IB // TP):
+            for ii in range(d * TP, (d + 1) * TP):
+                for h in range(HC // 128):
+                    at = slice(h * 128, (h + 1) * 128)
+                    acc = None
+                    for j in range(J):
+                        term = w2[pl.ds(ii * J + j, 1), at] * vals[h, pl.ds((j // R) * S * R + j % R, S, stride=R), :]
+                        acc = term if acc is None else acc + term
+                    part[i0 + ii, :, at] = acc
+
             @pl.when(d0 + d != c)
             def _():
                 part_copy(d0 + d, c).start()

time: 18.5 us -> 18.4 us (level)
  no operation moved by 1% of the time
where the time goes in v2:
time: 18.4 us; the launch traced here: 18.1 us
  Pallas kernels  17.5 us (95%)
  between operations  0.64 us (3%)
    pallas_call x1, Pallas kernels, on_device(): pl.pallas_call(functools.partial(kernel, (R, C, S, TP, I, J, IB)), out_sh...  16.2 us
    pallas_call x1, Pallas kernels, on_device(): pl.pallas_call(finish, out_shape=(jax.ShapeDtypeStruct((I * J, Z), f32),...  1.27 us

profile of v2, /device:TPU:0, one launch (start us, length us, event | category | flops | bytes accessed | tf_op | source)
XLA Modules:
  0.0 18.1 jit_solution(6642451479004649406)
XLA Ops:
  0.6 16.2 %msa_block.1 = (f32[128,128]{1,0:T(8,128)S(1)}, f32[32,256]{1,0:T(8,128)S(1)}, bf16[768,64]{1,0:T(8,128)(2,1)S(1)}, f32[32,64]{1,0:T(8,128)S(1)}) custom-call(f32[32,64]{1,0:T(8,128)} %bitcast.11, f32[128,128]{1,0:T(8,128)} %bitcast.9, f32[32,64]{1,0:T(8,128)} %bitcast.12, f32[32,64]{1,0:T(8,128)} %bitcast.13, f32[1024,128]{1,0:T(8,128)} %refs_4_.1, ...), custom_call_target="tpu_custom_call" | custom-call | tf_op jit(solution)/shard_map/msa_block/pallas_call | solution.py:332
  16.9 1.3 %msa_finish.1 = (f32[128,128]{1,0:T(8,128)}, f32[32,64]{1,0:T(8,128)}) custom-call(f32[128,128]{1,0:T(8,128)S(1)} %get-tuple-element.8.pair, f32[32,256]{1,0:T(8,128)S(1)} %get-tuple-element.9.mixed, bf16[768,64]{1,0:T(8,128)(2,1)S(1)} %get-tuple-element.10.mstk, f32[32,64]{1,0:T(8,128)S(1)} %get-tuple-element.11.x), custom_call_target="tpu_custom_call" | custom-call | tf_op jit(solution)/shard_map/msa_finish/pallas_call | solution.py:367
